TPU v7x, 256 devices: a whole 4x4x8 slice. The times are simulated.
256 devices in a mesh: dp: 32 (over z_lo, x, core), feat: 8 (over y, z_hi).
Axes of the slice: x: 4, y: 4, z: 8 (z_hi: 2, z_lo: 4; z = z_hi * 4 + z_lo), core: 2. Of those that a mesh axis runs over, the one named last changes fastest.
Arguments:
- view_a: bfloat16 [4096, 4096], P('dp', 'feat'), may hold values from -24 to 24
- view_b: bfloat16 [4096, 4096], P('dp', 'feat'), may hold values from -24 to 24
Outputs:
- grad_a: bfloat16 [4096, 4096], P('dp', 'feat')
- grad_b: bfloat16 [4096, 4096], P('dp', 'feat')
- loss: float32 [], replicated
All inputs are finite; a program needn't handle non-finite values.
Results may differ from a plain program's by a relative error of at most 0.0068.
Values may be sent and summed in bfloat16 or wider, within the bound.
A program may use at most 64 MiB of HBM per device.

v0:
```python
import jax
import jax.numpy as jnp
from jax import lax
from jax.sharding import Mesh
from jax.sharding import PartitionSpec as P

F = 4096
DP = ("dp_0", "dp_1", "dp_2")
FEAT = ("feat_0", "feat_1")
DP_FEAT = ("dp_0", "dp_1", "dp_2", "feat_0", "feat_1")
EPS = 1e-05
LAMBDA = 0.0051


def from_everyone(x, axis):
    copies = jnp.broadcast_to(x, (lax.axis_size(axis), *x.shape))
    return lax.all_to_all(copies, axis, split_axis=0, concat_axis=0, tiled=True)


def of_everyone(x, axis):
    return from_everyone(x, axis).sum(axis=0)


def in_one(arrays, axis):
    line, at, gathered = (jnp.concatenate([a.reshape(-1) for a in arrays]), 0, [])
    running = of_everyone(line, axis)
    for a in arrays:
        gathered.append(running[at : at + a.size].reshape(a.shape))
        at += a.size
    return tuple(gathered)


def joined_along(parts, dim):
    parts = jnp.moveaxis(parts, 0, dim)
    dims = parts.shape
    return parts.reshape(*dims[:dim], dims[dim] * dims[dim + 1], *dims[dim + 2 :])


def collect(x, axis, dim):
    parts = from_everyone(x, axis)
    return joined_along(parts, dim)


def split_up(x, dim, length):
    before, after = (x.shape[:dim], x.shape[dim + 1 :])
    return jnp.moveaxis(x.reshape(*before, length, -1, *after), dim, 0)


def scatter_pairs(x, chips, core, dim):
    sizes = (lax.axis_size(chips), lax.axis_size(core))
    parts = split_up(x, dim, sizes[0] * sizes[1])
    inside = parts.shape[1:]
    parts = parts.reshape(*sizes, *inside).swapaxes(0, 1).reshape(-1, *inside)
    parts = lax.psum_scatter(parts, core, scatter_dimension=0, tiled=True)
    return lax.psum_scatter(parts, chips, scatter_dimension=0, tiled=True)[0]


def over_axes(x, axes):
    for axis in axes:
        x = lax.psum(x, axis)
    return x


def shards(view_a, view_b):
    rows, local = view_a.shape
    groups = lax.axis_size(DP)
    count = rows * groups
    vals_a = view_a.astype(jnp.float32)
    vals_b = view_b.astype(jnp.float32)
    sums = in_one(
        (
            jnp.sum(vals_a, axis=0),
            jnp.sum(vals_a * vals_a, axis=0),
            jnp.sum(vals_b, axis=0),
            jnp.sum(vals_b * vals_b, axis=0),
        ),
        DP,
    )
    center_a = sums[0] / count
    center_b = sums[2] / count
    inverse_a = lax.rsqrt(sums[1] / count - center_a * center_a + EPS)
    inverse_b = lax.rsqrt(sums[3] / count - center_b * center_b + EPS)
    normed_a = (vals_a - center_a) * inverse_a
    normed_b = (vals_b - center_b) * inverse_b
    a_half = normed_a.astype(jnp.bfloat16)
    b_half = normed_b.astype(jnp.bfloat16)
    b_every = collect(b_half, FEAT, 1)
    block_rows = F // groups
    corr_t = (
        scatter_pairs(
            lax.dot_general(
                b_every, a_half, (((0,), (0,)), ((), ())), preferred_element_type=jnp.float32
            ),
            ("dp_0", "dp_1"),
            "dp_2",
            0,
        )
        / count
    )
    row_ids = lax.axis_index(DP) * block_rows + lax.broadcasted_iota(
        jnp.int32, (block_rows, local), 0
    )
    col_ids = lax.axis_index(FEAT) * local + lax.broadcasted_iota(jnp.int32, (block_rows, local), 1)
    unit = (row_ids == col_ids).astype(jnp.float32)
    partial_loss = jnp.sum(unit * (1.0 - corr_t) ** 2) + LAMBDA * jnp.sum(
        (1.0 - unit) * corr_t * corr_t
    )
    loss = over_axes(partial_loss, DP_FEAT) / F
    grad_t = (unit * (-2.0 * (1.0 - corr_t)) + (1.0 - unit) * (2.0 * LAMBDA) * corr_t).astype(
        jnp.bfloat16
    )
    grad_full = lax.all_gather(grad_t, DP, axis=0, tiled=True)
    grad_na = jnp.dot(b_every, grad_full, preferred_element_type=jnp.float32)
    partial_b = lax.dot_general(
        a_half, grad_full, (((1,), (1,)), ((), ())), preferred_element_type=jnp.float32
    )
    grad_nb = lax.psum_scatter(partial_b, FEAT, scatter_dimension=1, tiled=True)
    stats = in_one(
        (
            jnp.sum(grad_na, axis=0),
            jnp.sum(grad_na * normed_a, axis=0),
            jnp.sum(grad_nb, axis=0),
            jnp.sum(grad_nb * normed_b, axis=0),
        ),
        DP,
    )
    grad_a = (inverse_a * (grad_na - stats[0] / count - normed_a * (stats[1] / count))).astype(
        jnp.bfloat16
    )
    grad_b = (inverse_b * (grad_nb - stats[2] / count - normed_b * (stats[3] / count))).astype(
        jnp.bfloat16
    )
    return (grad_a, grad_b, loss)


def solution(mesh):
    torus = Mesh(mesh.devices.reshape(4, 4, 2, 4, 2), ("dp_0", "dp_1", "dp_2", "feat_0", "feat_1"))
    in_specs = (P(DP, FEAT), P(DP, FEAT))
    out_specs = (P(DP, FEAT), P(DP, FEAT), P())
    return jax.shard_map(
        shards, mesh=torus, in_specs=in_specs, out_specs=out_specs, check_vma=False
    )
```

profile of v0, /device:TPU:0, one launch (start us, length us, event | category | flops | bytes accessed | tf_op | source)
XLA Modules:
  0.0 412.7 jit_solution(12478503057353456559)
XLA Ops:
  7.2 0.0 copy-start
  7.2 0.0 reduce-scatter.4.cloned.1.call-start
  7.2 1.1 convert_reduce_fusion
  8.3 0.1 broadcast_in_dim.6
  8.5 17.9 %all_to_all.17 = f32[32,1,2048]{2,1,0:T(1,128)S(1)} all-to-all(f32[32,1,2048]{2,1,0:T(1,128)S(1)} %broadcast_in_dim.6), channel_id=1, replica_groups=mesh['dp_0'=4,'dp_1'=4,'dp_2'=2,'feat_0'=4,'feat_1'=2] {'dp_0','dp_1','d..., dimensions={0} | all-to-all | bytes 524288 | tf_op jit(solution)/shard_map/all_to_all | solution.py:17
  26.4 0.2 reduce_sum.112
  26.6 0.9 fusion.13
  27.5 0.1 copy.11
  27.6 0.1 broadcast_in_dim.7
  27.8 34.1 %all_to_all.18 = bf16[8,128,512]{1,2,0:T(8,128)(2,1)S(1)} all-to-all(bf16[8,128,512]{1,2,0:T(8,128)(2,1)S(1)} %broadcast_in_dim.7), channel_id=1, replica_groups=mesh['dp_0'=4,'dp_1'=4,'dp_2'=2,'feat_0'=4,'feat_1'=2] {'feat_0','feat_1'}, dimensions={0} | all-to-all | bytes 2097152 | tf_op jit(solution)/shard_map/all_to_all | solution.py:17
  61.9 0.0 copy-done
  61.9 1.3 convolution_bitcast_fusion
  63.1 4.2 %copy.12 = f32[2,16,128,512]{3,2,1,0:T(8,128)} copy(f32[2,16,128,512]{3,2,0,1:T(8,128)S(1)} %convolution_bitcast_fusion) | data formatting | bytes 16777216 | tf_op jit(solution)/shard_map/transpose | solution.py:53
  67.4 0.0 reduce-scatter.4.cloned.1.call-update
  67.4 0.0 reduce-scatter.6.cloned.1.call-start
  67.5 19.9 %reduce-scatter.4.cloned.1.call-done = f32[16,128,512]{2,1,0:T(8,128)} async-done(((f32[32,128,512]{2,1,0:T(8,128)}), f32[16,128,512]{2,1,0:T(8,128)}) %reduce-scatter.4.cloned.1.call-update) | async-done | bytes 4194320 | tf_op jit(solution)/shard_map/reduce_scatter | solution.py:54
  87.4 0.0 reduce-scatter.6.cloned.1.call-update
  87.4 0.0 all-gather.2.cloned.1.call-start
  87.5 98.5 %reduce-scatter.6.cloned.1.call-done = f32[1,128,512]{2,1,0:T(8,128)} async-done(((f32[16,128,512]{2,1,0:T(8,128)}), f32[1,128,512]{2,1,0:T(8,128)}) %reduce-scatter.6.cloned.1.call-update) | async-done | bytes 262160 | tf_op jit(solution)/shard_map/reduce_scatter | solution.py:55
  186.0 2.4 fusion.18
  188.4 0.0 all-gather.2.cloned.1.call-update
  188.4 0.0 reduce-scatter.8.cloned.1.call-start
  188.5 58.6 %all-gather.2.cloned.1.call-done = bf16[4096,512]{1,0:T(8,128)(2,1)} async-done(((bf16[128,512]{1,0:T(8,128)(2,1)}), bf16[4096,512]{1,0:T(8,128)(2,1)}) %all-gather.2.cloned.1.call-update) | async-done | bytes 4194320 | tf_op jit(solution)/shard_map/all_gather | solution.py:112
  247.1 5.0 %fusion.26 = f32[128,4096]{1,0:T(8,128)} fusion(bf16[4096,512]{1,0:T(8,128)(2,1)} %all-gather.2.cloned.1.call-done, bf16[128,512]{1,0:T(8,128)(2,1)S(1)} %copy-done, f32[512]{0:T(512)S(1)} %get-tuple-element.20, f32[512]{0:T(512)S(1)} %get-tuple-element.18), kind=kOutput, calls=%fused_computation.38 | convolution fusion | flops 537133056 | bytes 6426624 | tf_op jit(solution)/shard_map/dot_general | solution.py:114
  252.1 0.0 copy-start.1
  252.1 0.0 reduce-scatter.8.cloned.1.call-update
  252.1 3.0 fusion.35
  255.1 91.8 %reduce-scatter.8.cloned.1.call-done = f32[128,512]{1,0:T(8,128)} async-done(((f32[128,4096]{1,0:T(8,128)}), f32[128,512]{1,0:T(8,128)}) %reduce-scatter.8.cloned.1.call-update) | async-done | bytes 262160 | tf_op jit(solution)/shard_map/reduce_scatter | solution.py:117
  346.9 0.0 copy-done.1
  346.9 1.0 fusion.36
  347.9 0.8 broadcast_in_dim.8
  348.8 4.9 %all-to-all-start.2 = ((f32[32,1,2048]{2,1,0:T(1,128)}), f32[32,1,2048]{2,1,0:T(1,128)S(1)}, u32[]{:S(2)}, u32[]{:S(2)}) async-start(f32[32,1,2048]{2,1,0:T(1,128)} %broadcast_in_dim.8), calls=%async_computation.5 | async-start | bytes 524288 | tf_op jit(solution)/shard_map/all_to_all | solution.py:17
  355.0 12.5 %psum.35 = f32[]{:T(128)} all-reduce(f32[]{:T(128)S(6)} %add.61), channel_id=1, replica_groups=mesh['dp_0'=4,'dp_1'=4,'dp_2'=2,'feat_0'=4,'feat_1'=2] {'dp_0'}, use_global_device_ids=true, to_apply=%region_15.0 | all-reduce | flops 1 | bytes 8 | tf_op jit(solution)/shard_map/psum | solution.py:60
  367.5 11.0 %psum.36 = f32[]{:T(128)} all-reduce(f32[]{:T(128)} %psum.35), channel_id=1, replica_groups=mesh['dp_0'=4,'dp_1'=4,'dp_2'=2,'feat_0'=4,'feat_1'=2] {'dp_1'}, use_global_device_ids=true, to_apply=%region_16.0 | all-reduce | flops 1 | bytes 8 | tf_op jit(solution)/shard_map/psum | solution.py:60
  378.5 3.1 psum.37
  381.6 10.7 %psum.38 = f32[]{:T(128)} all-reduce(f32[]{:T(128)} %psum.37), channel_id=1, replica_groups=mesh['dp_0'=4,'dp_1'=4,'dp_2'=2,'feat_0'=4,'feat_1'=2] {'feat_0'}, use_global_device_ids=true, to_apply=%region_18.0 | all-reduce | flops 1 | bytes 8 | tf_op jit(solution)/shard_map/psum | solution.py:60
  392.4 9.4 %psum.39 = f32[]{:T(128)} all-reduce(f32[]{:T(128)} %psum.38), channel_id=1, replica_groups=mesh['dp_0'=4,'dp_1'=4,'dp_2'=2,'feat_0'=4,'feat_1'=2] {'feat_1'}, use_global_device_ids=true, to_apply=%region_19.0 | all-reduce | flops 1 | bytes 8 | tf_op jit(solution)/shard_map/psum | solution.py:60
  402.5 0.0 all-to-all-done.2
  402.5 0.2 reduce_sum.117
  402.7 0.7 fusion.8
  403.4 1.7 fusion.17
  (6 shorter events, 0.0 us)
Async XLA Ops:
  7.2 54.7 %copy-start = (bf16[128,512]{1,0:T(8,128)(2,1)S(1)}, bf16[128,512]{1,0:T(8,128)(2,1)}, u32[]{:S(2)}) copy-start(bf16[128,512]{1,0:T(8,128)(2,1)} %param.2) | copy-start | bytes 393220
  7.2 80.2 %reduce-scatter.4.cloned.1.call-start = ((), (), s32[]{:S(2)}) async-start(), calls=%async_computation.6 | async-start | bytes 12582912 | tf_op jit(solution)/shard_map/reduce_scatter | solution.py:54
  67.4 118.6 %reduce-scatter.6.cloned.1.call-start = ((), (), s32[]{:S(2)}) async-start(), calls=%async_computation.7 | async-start | bytes 4456448 | tf_op jit(solution)/shard_map/reduce_scatter | solution.py:55
  87.4 159.7 %all-gather.2.cloned.1.call-start = ((), (), s32[]{:S(2)}) async-start(), calls=%async_computation.8 | async-start | bytes 4325376 | tf_op jit(solution)/shard_map/all_gather | solution.py:112
  188.4 158.5 %reduce-scatter.8.cloned.1.call-start = ((), (), s32[]{:S(2)}) async-start(), calls=%async_computation.9 | async-start | bytes 2359296 | tf_op jit(solution)/shard_map/reduce_scatter | solution.py:117
  252.1 94.8 %copy-start.1 = (bf16[128,512]{1,0:T(8,128)(2,1)S(1)}, bf16[128,512]{1,0:T(8,128)(2,1)}, u32[]{:S(2)}) copy-start(bf16[128,512]{1,0:T(8,128)(2,1)} %param.3) | copy-start | bytes 393220
  348.8 53.7 %all-to-all-start.2 = ((f32[32,1,2048]{2,1,0:T(1,128)}), f32[32,1,2048]{2,1,0:T(1,128)S(1)}, u32[]{:S(2)}, u32[]{:S(2)}) async-start(f32[32,1,2048]{2,1,0:T(1,128)} %broadcast_in_dim.8), calls=%async_computation.5 | async-start | bytes 524288 | tf_op jit(solution)/shard_map/all_to_all | solution.py:17
Sparse Core Ops, SparseCore 0:
  67.5 19.8 reduce-scatter.3
  89.9 96.0 reduce-scatter.5
  188.6 58.5 all-gather.1
  252.3 94.5 reduce-scatter.7
where the time goes:
time: 413 us
  waiting for transfers between devices  269 us (65%)
  blocking collectives  98.9 us (24%)
  between operations  17 us (4%)
  matrix products  9.23 us (2%)
  other arithmetic  8.25 us (2%)
  local copies, waits for them, and re-layouts  5.46 us (1%)
  starting transfers between devices  5.08 us (1%)
    reduce_scatter x1, waiting for transfers between devices, scatter_pairs(): return lax.psum_scatter(parts, chips, scatter_dimension=0, tiled=True)[0]  98.5 us
    reduce_scatter x1, waiting for transfers between devices, shards(): grad_nb = lax.psum_scatter(partial_b, FEAT, scatter_dimension=1, tiled=True)  91.8 us
    all_gather x1, waiting for transfers between devices, shards(): grad_full = lax.all_gather(grad_t, DP, axis=0, tiled=True)  58.6 us
    all_to_all x2, blocking collectives, from_everyone(): return lax.all_to_all(copies, axis, split_axis=0, concat_axis=0, tiled=True)  52 us
    psum x5, blocking collectives, over_axes(): x = lax.psum(x, axis)  46.8 us
    reduce_scatter x1, waiting for transfers between devices, scatter_pairs(): parts = lax.psum_scatter(parts, core, scatter_dimension=0, tiled=True)  19.9 us
  transfers between devices with their start and end apart: 5, of which 4 were waited for; matrix products, arithmetic and copies ran while one was open for 1% of the time, Pallas kernels for 0%

commit v1 on v0

--- a/solution.py
+++ b/solution.py
@@ -109,7 +109,8 @@
     grad_t = (unit * (-2.0 * (1.0 - corr_t)) + (1.0 - unit) * (2.0 * LAMBDA) * corr_t).astype(
         jnp.bfloat16
     )
-    grad_full = lax.all_gather(grad_t, DP, axis=0, tiled=True)
+    sent = jnp.stack([grad_t] * lax.axis_size(DP))
+    grad_full = jnp.concatenate(lax.all_to_all(sent, DP, 0, 0), axis=0)
     grad_na = jnp.dot(b_every, grad_full, preferred_element_type=jnp.float32)
     partial_b = lax.dot_general(
         a_half, grad_full, (((1,), (1,)), ((), ())), preferred_element_type=jnp.float32

time: 413 us -> 452 us (1.094)
  blocking collectives: 98.9 us -> 196 us
  waiting for transfers between devices: 269 us -> 211 us
    all_to_all x0 -> x1, blocking collectives: none -> 96.7 us  [shards(): grad_full = jnp.concatenate(lax.all_to_all(sent, DP, 0, 0), axis=0)]
    all_gather x1 -> x0, waiting for transfers between devices: 58.6 us -> none  [shards(): grad_full = lax.all_gather(grad_t, DP, axis=0, tiled=True)]
  transfers between devices with their start and end apart: 5 -> 4, of which waited for: 4 -> 3; matrix products, arithmetic and copies ran while one was open for 1% -> 1% of each run, Pallas kernels for 0% -> 0%
where the time goes in v1:
time: 452 us
  waiting for transfers between devices  211 us (47%)
  blocking collectives  196 us (43%)
  between operations  17 us (4%)
  local copies, waits for them, and re-layouts  7.85 us (2%)
  other arithmetic  7.73 us (2%)
  matrix products  7.07 us (2%)
  starting transfers between devices  5.01 us (1%)
    reduce_scatter x1, waiting for transfers between devices, scatter_pairs(): return lax.psum_scatter(parts, chips, scatter_dimension=0, tiled=True)[0]  98.5 us
    all_to_all x1, blocking collectives, shards(): grad_full = jnp.concatenate(lax.all_to_all(sent, DP, 0, 0), axis=0)  96.7 us
    reduce_scatter x1, waiting for transfers between devices, shards(): grad_nb = lax.psum_scatter(partial_b, FEAT, scatter_dimension=1, tiled=True)  92.9 us
    all_to_all x2, blocking collectives, from_everyone(): return lax.all_to_all(copies, axis, split_axis=0, concat_axis=0, tiled=True)  52 us
    psum x5, blocking collectives, over_axes(): x = lax.psum(x, axis)  46.8 us
    reduce_scatter x1, waiting for transfers between devices, scatter_pairs(): parts = lax.psum_scatter(parts, core, scatter_dimension=0, tiled=True)  19.9 us
  transfers between devices with their start and end apart: 4, of which 3 were waited for; matrix products, arithmetic and copies ran while one was open for 1% of the time, Pallas kernels for 0%

profile of v1, /device:TPU:0, one launch (start us, length us, event | category | flops | bytes accessed | tf_op | source)
XLA Modules:
  0.0 451.6 jit_solution(17510807596026867051)
XLA Ops:
  7.2 0.0 copy-start.1
  7.2 0.0 reduce-scatter.4.cloned.1.call-start
  7.2 1.1 convert_reduce_fusion
  8.3 0.1 broadcast_in_dim.6
  8.5 17.9 %all_to_all.22 = f32[32,1,2048]{2,1,0:T(1,128)S(1)} all-to-all(f32[32,1,2048]{2,1,0:T(1,128)S(1)} %broadcast_in_dim.6), channel_id=1, replica_groups=mesh['dp_0'=4,'dp_1'=4,'dp_2'=2,'feat_0'=4,'feat_1'=2] {'dp_0','dp_1','d..., dimensions={0} | all-to-all | bytes 524288 | tf_op jit(solution)/shard_map/all_to_all | solution.py:17
  26.4 0.2 reduce_sum.112
  26.6 0.9 fusion.20
  27.5 0.1 copy.11
  27.6 0.1 broadcast_in_dim.7
  27.8 34.1 %all_to_all.23 = bf16[8,128,512]{1,2,0:T(8,128)(2,1)S(1)} all-to-all(bf16[8,128,512]{1,2,0:T(8,128)(2,1)S(1)} %broadcast_in_dim.7), channel_id=1, replica_groups=mesh['dp_0'=4,'dp_1'=4,'dp_2'=2,'feat_0'=4,'feat_1'=2] {'feat_0','feat_1'}, dimensions={0} | all-to-all | bytes 2097152 | tf_op jit(solution)/shard_map/all_to_all | solution.py:17
  61.9 0.0 copy-done.1
  61.9 1.3 convolution_bitcast_fusion
  63.1 4.2 copy.12
  67.4 0.0 reduce-scatter.4.cloned.1.call-update
  67.4 0.0 reduce-scatter.6.cloned.1.call-start
  67.5 19.9 %reduce-scatter.4.cloned.1.call-done = f32[16,128,512]{2,1,0:T(8,128)} async-done(((f32[32,128,512]{2,1,0:T(8,128)}), f32[16,128,512]{2,1,0:T(8,128)}) %reduce-scatter.4.cloned.1.call-update) | async-done | bytes 4194320 | tf_op jit(solution)/shard_map/reduce_scatter | solution.py:54
  87.4 0.0 reduce-scatter.6.cloned.1.call-update
  87.4 0.0 reduce-scatter.8.cloned.1.call-start
  87.5 98.5 %reduce-scatter.6.cloned.1.call-done = f32[1,128,512]{2,1,0:T(8,128)} async-done(((f32[16,128,512]{2,1,0:T(8,128)}), f32[1,128,512]{2,1,0:T(8,128)}) %reduce-scatter.6.cloned.1.call-update) | async-done | bytes 262160 | tf_op jit(solution)/shard_map/reduce_scatter | solution.py:55
  186.0 1.1 fusion.28
  187.1 0.5 stack.5
  187.6 96.7 %all_to_all.24 = bf16[32,128,512]{2,1,0:T(8,128)(2,1)S(1)} all-to-all(bf16[32,128,512]{2,1,0:T(8,128)(2,1)S(1)} %stack.5), channel_id=1, replica_groups=mesh['dp_0'=4,'dp_1'=4,'dp_2'=2,'feat_0'=4,'feat_1'=2] {'dp_0','dp_1','d..., dimensions={0} | all-to-all | bytes 8388608 | tf_op jit(solution)/shard_map/all_to_all | solution.py:113
  284.2 0.0 copy-start
  284.2 1.9 copy-done
  286.2 2.8 fusion.29
  289.0 0.0 copy-start.2
  289.0 0.0 copy-start.3
  289.0 0.0 reduce-scatter.8.cloned.1.call-update
  289.0 3.0 fusion.38
  292.0 92.9 %reduce-scatter.8.cloned.1.call-done = f32[128,512]{1,0:T(8,128)} async-done(((f32[128,4096]{1,0:T(8,128)}), f32[128,512]{1,0:T(8,128)}) %reduce-scatter.8.cloned.1.call-update) | async-done | bytes 262160 | tf_op jit(solution)/shard_map/reduce_scatter | solution.py:118
  384.9 0.0 copy-done.2
  384.9 1.0 fusion.39
  386.0 0.8 broadcast_in_dim.8
  386.8 4.9 %all-to-all-start.3 = ((f32[32,1,2048]{2,1,0:T(1,128)}), f32[32,1,2048]{2,1,0:T(1,128)S(1)}, u32[]{:S(2)}, u32[]{:S(2)}) async-start(f32[32,1,2048]{2,1,0:T(1,128)} %broadcast_in_dim.8), calls=%async_computation.6 | async-start | bytes 524288 | tf_op jit(solution)/shard_map/all_to_all | solution.py:17
  391.7 0.0 copy-done.3
  391.7 0.8 fusion.25
  393.8 12.5 %psum.35 = f32[]{:T(128)} all-reduce(f32[]{:T(128)S(6)} %add.62), channel_id=1, replica_groups=mesh['dp_0'=4,'dp_1'=4,'dp_2'=2,'feat_0'=4,'feat_1'=2] {'dp_0'}, use_global_device_ids=true, to_apply=%region_15.0 | all-reduce | flops 1 | bytes 8 | tf_op jit(solution)/shard_map/psum | solution.py:60
  406.3 11.0 %psum.36 = f32[]{:T(128)} all-reduce(f32[]{:T(128)} %psum.35), channel_id=1, replica_groups=mesh['dp_0'=4,'dp_1'=4,'dp_2'=2,'feat_0'=4,'feat_1'=2] {'dp_1'}, use_global_device_ids=true, to_apply=%region_16.0 | all-reduce | flops 1 | bytes 8 | tf_op jit(solution)/shard_map/psum | solution.py:60
  417.4 3.1 psum.37
  420.5 10.7 %psum.38 = f32[]{:T(128)} all-reduce(f32[]{:T(128)} %psum.37), channel_id=1, replica_groups=mesh['dp_0'=4,'dp_1'=4,'dp_2'=2,'feat_0'=4,'feat_1'=2] {'feat_0'}, use_global_device_ids=true, to_apply=%region_18.0 | all-reduce | flops 1 | bytes 8 | tf_op jit(solution)/shard_map/psum | solution.py:60
  431.2 9.4 %psum.39 = f32[]{:T(128)} all-reduce(f32[]{:T(128)} %psum.38), channel_id=1, replica_groups=mesh['dp_0'=4,'dp_1'=4,'dp_2'=2,'feat_0'=4,'feat_1'=2] {'feat_1'}, use_global_device_ids=true, to_apply=%region_19.0 | all-reduce | flops 1 | bytes 8 | tf_op jit(solution)/shard_map/psum | solution.py:60
  441.3 0.0 all-to-all-done.3
  441.3 0.2 reduce_sum.117
  441.5 0.7 fusion.15
  442.2 1.7 fusion.24
  (6 shorter events, 0.0 us)
Async XLA Ops:
  7.2 54.7 %copy-start.1 = (bf16[128,512]{1,0:T(8,128)(2,1)S(1)}, bf16[128,512]{1,0:T(8,128)(2,1)}, u32[]{:S(2)}) copy-start(bf16[128,512]{1,0:T(8,128)(2,1)} %param.2) | copy-start | bytes 393220
  7.2 80.2 %reduce-scatter.4.cloned.1.call-start = ((), (), s32[]{:S(2)}) async-start(), calls=%async_computation.7 | async-start | bytes 12582912 | tf_op jit(solution)/shard_map/reduce_scatter | solution.py:54
  67.4 118.6 %reduce-scatter.6.cloned.1.call-start = ((), (), s32[]{:S(2)}) async-start(), calls=%async_computation.8 | async-start | bytes 4456448 | tf_op jit(solution)/shard_map/reduce_scatter | solution.py:55
  87.4 297.5 %reduce-scatter.8.cloned.1.call-start = ((), (), s32[]{:S(2)}) async-start(), calls=%async_computation.9 | async-start | bytes 2359296 | tf_op jit(solution)/shard_map/reduce_scatter | solution.py:118
  284.2 1.9 copy-start
  289.0 96.0 %copy-start.2 = (bf16[128,512]{1,0:T(8,128)(2,1)S(1)}, bf16[128,512]{1,0:T(8,128)(2,1)}, u32[]{:S(2)}) copy-start(bf16[128,512]{1,0:T(8,128)(2,1)} %param.3) | copy-start | bytes 393220
  289.0 102.7 %copy-start.3 = (f32[1,128,512]{2,1,0:T(8,128)S(1)}, f32[1,128,512]{2,1,0:T(8,128)}, u32[]{:S(2)}) copy-start(f32[1,128,512]{2,1,0:T(8,128)} %reduce-scatter.6.cloned.1.call-done) | copy-start | bytes 786436
  386.8 54.5 %all-to-all-start.3 = ((f32[32,1,2048]{2,1,0:T(1,128)}), f32[32,1,2048]{2,1,0:T(1,128)S(1)}, u32[]{:S(2)}, u32[]{:S(2)}) async-start(f32[32,1,2048]{2,1,0:T(1,128)} %broadcast_in_dim.8), calls=%async_computation.6 | async-start | bytes 524288 | tf_op jit(solution)/shard_map/all_to_all | solution.py:17
Sparse Core Ops, SparseCore 0:
  67.5 19.8 reduce-scatter.3
  89.9 96.0 reduce-scatter.5
  289.1 95.7 reduce-scatter.7
